TPU v7x, 32 devices: a whole 2x2x4 slice. The times are simulated.
32 devices in a mesh: fsdp: 4 (over y, x), ep: 8 (over z, core).
Axes of the slice: x: 2, y: 2, z: 4, core: 2. Of those that a mesh axis runs over, the one named last changes fastest.
Arguments:
- hidden_in: bfloat16 [8192, 2048], P(('fsdp', 'ep')), may hold values from -6 to 6
- norm_gain: float32 [2048], replicated, may hold values from 0.25 to 1.75
- expert_ids: int32 [8192, 8], P(('fsdp', 'ep')), may hold values from 0 to 15, all different within a row; in each aligned block of 256 rows (0 to 255, 256 to 511, ...) at most 160 rows name the same one
- expert_probs: float32 [8192, 8], P(('fsdp', 'ep')), may hold values from 0.05 to 0.25
- gate_proj: bfloat16 [16, 2048, 768], P('ep', 'fsdp'), may hold values from -0.125 to 0.125
- up_proj: bfloat16 [16, 2048, 768], P('ep', 'fsdp'), may hold values from -0.125 to 0.125
- down_proj: bfloat16 [16, 768, 2048], P('ep', None, 'fsdp'), may hold values from -0.21875 to 0.21875
Outputs:
- moe_out: bfloat16 [8192, 2048], P(('fsdp', 'ep'))
Inputs may be any that keep to these rules, and one draw needn't show every extreme that they name: `expert_ids`: within the rows of one device (aligned blocks of 256 rows) each expert id is named by at most 160 rows, and in some blocks one expert by exactly 160; the 8 ids of a row are distinct.
All inputs are finite; a program needn't handle non-finite values.
Results may differ from a plain program's by a relative error of at most 0.0025.
Values may be sent and summed in bfloat16 or wider, within the bound.
A program may use at most 128 MiB of HBM per device.

v0:
```python
import jax
import jax.numpy as jnp
from jax import lax
from jax.sharding import PartitionSpec as P


def rms_norm(hidden_in, norm_gain):
    values = hidden_in.astype(jnp.float32)
    spread = jnp.mean(values * values, axis=-1, keepdims=True)
    return (values * lax.rsqrt(spread + 1e-06) * norm_gain).astype(jnp.bfloat16)


def per_device(hidden_in, norm_gain, expert_ids, expert_probs, gate_proj, up_proj, down_proj):
    local_experts = gate_proj.shape[0]
    normed = rms_norm(hidden_in, norm_gain)
    all_experts = local_experts * lax.axis_size("ep")
    hot = expert_ids[:, :, None] == jnp.arange(all_experts, dtype=jnp.int32)
    weights = jnp.sum(jnp.where(hot, expert_probs[:, :, None], 0.0), axis=1)
    tokens = lax.all_gather(normed, "ep", axis=0, tiled=True)
    routed = lax.all_to_all(
        weights.reshape(weights.shape[0], lax.axis_size("ep"), local_experts),
        "ep",
        split_axis=1,
        concat_axis=0,
        tiled=True,
    ).reshape(tokens.shape[0], local_experts)
    total = 0.0
    gate_all = lax.all_gather(gate_proj, "fsdp", axis=1, tiled=True)
    up_all = lax.all_gather(up_proj, "fsdp", axis=1, tiled=True)
    down_all = lax.all_gather(down_proj, "fsdp", axis=2, tiled=True)
    for e in range(local_experts):
        gate = jnp.dot(tokens, gate_all[e], preferred_element_type=jnp.float32)
        up = jnp.dot(tokens, up_all[e], preferred_element_type=jnp.float32)
        act = (jax.nn.silu(gate) * up).astype(jnp.bfloat16)
        out = jnp.dot(act, down_all[e], preferred_element_type=jnp.float32).astype(jnp.bfloat16)
        total = total + out.astype(jnp.float32) * routed[:, e, None]
    combined = lax.psum_scatter(total, "ep", scatter_dimension=0, tiled=True)
    return combined.astype(jnp.bfloat16)


def solution(mesh):
    return jax.shard_map(
        per_device,
        mesh=mesh,
        in_specs=(
            P(("fsdp", "ep"), None),
            P(),
            P(("fsdp", "ep"), None),
            P(("fsdp", "ep"), None),
            P("ep", "fsdp", None),
            P("ep", "fsdp", None),
            P("ep", None, "fsdp"),
        ),
        out_specs=P(("fsdp", "ep"), None),
        check_vma=False,
    )
```

profile of v0, /device:TPU:0, one launch (start us, length us, event | category | flops | bytes accessed | tf_op | source)
XLA Modules:
  0.0 533.1 jit_solution(4729882364466384271)
XLA Ops:
  6.5 0.0 copy-start
  6.5 0.0 copy-start.1
  6.5 0.0 all-gather.7.cloned.1.call-start
  6.5 0.7 all-gather.7.cloned.1.call-update
  7.3 0.0 all-gather.5.cloned.1.call-start
  7.3 1.5 fusion.5
  8.8 2.5 fusion.7
  11.3 0.0 all-gather.5.cloned.1.call-update
  11.4 0.0 all-gather.9.cloned.1.call-start
  11.4 0.7 all-gather.9.cloned.1.call-update
  12.1 0.0 all-gather.11.cloned.1.call-start
  12.1 0.5 all-gather.11.cloned.1.call-update
  12.7 0.0 reduce-scatter.2.cloned.1.call-start
  12.7 0.0 copy-done
  12.7 0.0 copy-done.1
  12.8 11.8 %all_to_all.15 = f32[256,8,2]{0,2,1:T(2,128)S(1)} all-to-all(f32[256,8,2]{0,2,1:T(2,128)S(1)} %reshape.18), channel_id=1, replica_groups=mesh['fsdp'=4,'ep'=8] {'ep'}, dimensions={1} | all-to-all | bytes 32768 | tf_op jit(solution)/shard_map/all_to_all | solution.py:20
  24.6 57.4 %all-gather.7.cloned.1.call-done = bf16[2,2048,768]{2,1,0:T(8,128)(2,1)} async-done(((bf16[2,512,768]{2,1,0:T(8,128)(2,1)}), bf16[2,2048,768]{2,1,0:T(8,128)(2,1)}) %all-gather.7.cloned.1.call-update) | async-done | bytes 6291472 | tf_op jit(solution)/shard_map/all_gather | solution.py:28
  82.0 83.7 %all-gather.5.cloned.1.call-done = bf16[2048,2048]{1,0:T(8,128)(2,1)} async-done(((bf16[256,2048]{1,0:T(8,128)(2,1)}), bf16[2048,2048]{1,0:T(8,128)(2,1)}) %all-gather.5.cloned.1.call-update) | async-done | bytes 8388624 | tf_op jit(solution)/shard_map/all_gather | solution.py:19
  165.6 0.0 copy-start.2
  165.6 0.0 copy-start.3
  165.6 11.8 %fusion.1 = f32[2048,768]{1,0:T(8,128)} fusion(bf16[2048,2048]{1,0:T(8,128)(2,1)} %all-gather.5.cloned.1.call-done, bf16[2,2048,768]{2,1,0:T(8,128)(2,1)} %all-gather.7.cloned.1.call-done), kind=kOutput, calls=%fused_computation.7 | convolution fusion | flops 6442450944 | bytes 17825792 | tf_op jit(solution)/shard_map/dot_general | solution.py:32
  177.4 0.0 copy-done.2
  177.4 0.0 copy-done.3
  177.4 8.5 %fusion.2 = f32[2048,768]{1,0:T(8,128)} fusion(bf16[2048,2048]{1,0:T(8,128)(2,1)S(1)} %copy-done.2, bf16[2,2048,768]{2,1,0:T(8,128)(2,1)S(1)} %copy-done.3), kind=kOutput, calls=%fused_computation.11 | convolution fusion | flops 6442450944 | bytes 17825792 | tf_op jit(solution)/shard_map/dot_general | solution.py:32
  185.9 50.1 %all-gather.9.cloned.1.call-done = bf16[2,2048,768]{2,1,0:T(8,128)(2,1)} async-done(((bf16[2,512,768]{2,1,0:T(8,128)(2,1)}), bf16[2,2048,768]{2,1,0:T(8,128)(2,1)}) %all-gather.9.cloned.1.call-update) | async-done | bytes 6291472 | tf_op jit(solution)/shard_map/all_gather | solution.py:29
  236.0 71.6 %all-gather.11.cloned.1.call-done = bf16[2,768,2048]{2,1,0:T(8,128)(2,1)} async-done(((bf16[2,768,512]{2,1,0:T(8,128)(2,1)}), bf16[2,768,2048]{2,1,0:T(8,128)(2,1)}) %all-gather.11.cloned.1.call-update) | async-done | bytes 6291472 | tf_op jit(solution)/shard_map/all_gather | solution.py:30
  307.6 22.1 %fusion = bf16[2048,2048]{1,0:T(8,128)(2,1)} fusion(f32[2048,768]{1,0:T(8,128)} %fusion.2, bf16[2048,2048]{1,0:T(8,128)(2,1)} %all-gather.5.cloned.1.call-done, bf16[2,768,2048]{2,1,0:T(8,128)(2,1)} %all-gather.11.cloned.1.call-done, bf16[2,2048,768]{2,1,0:T(8,128)(2,1)} %all-gather.9.cloned.1.call-done), kind=kOutput, calls=%fused_computation.3 | convolution fusion | flops 12894339072 | bytes 29360128 | tf_op jit(solution)/shard_map/dot_general | solution.py:35
  329.7 25.8 %multiply_add_fusion = f32[2048,2048]{1,0:T(8,128)} fusion(f32[2048]{0:T(1024)S(1)} %bitcast.35, f32[2048]{0:T(1024)S(1)} %bitcast.34, bf16[2048,2048]{1,0:T(8,128)(2,1)} %fusion, f32[2048,768]{1,0:T(8,128)} %fusion.1, bf16[2048,2048]{1,0:T(8,128)(2,1)} %all-gather.5.cloned.1.call-done, bf16[2,768,2048]{2,1,0:T(8,128)(2,1)} %all-gather.11.cloned.1.call-done, ...), kind=kOutput, calls=%fused_computation | convolution fusion | flops 12919504896 | bytes 46153728 | tf_op jit(solution)/shard_map/dot_general | solution.py:35
  355.5 0.0 reduce-scatter.2.cloned.1.call-update
  355.5 168.3 %reduce-scatter.2.cloned.1.call-done = f32[256,2048]{1,0:T(8,128)} async-done(((f32[2048,2048]{1,0:T(8,128)}), f32[256,2048]{1,0:T(8,128)}) %reduce-scatter.2.cloned.1.call-update) | async-done | bytes 2097168 | tf_op jit(solution)/shard_map/reduce_scatter | solution.py:37
  523.8 2.7 convert_element_type.35
  (4 shorter events, 0.1 us)
Async XLA Ops:
  6.5 6.2 %copy-start = (f32[256,8]{0,1:T(8,128)S(1)}, f32[256,8]{0,1:T(8,128)}, u32[]{:S(2)}) copy-start(f32[256,8]{0,1:T(8,128)} %param.10) | copy-start | bytes 24580
  6.5 6.2 %copy-start.1 = (s32[256,8]{0,1:T(8,128)S(1)}, s32[256,8]{0,1:T(8,128)}, u32[]{:S(2)}) copy-start(s32[256,8]{0,1:T(8,128)} %param.9) | copy-start | bytes 24580
  6.5 75.4 %all-gather.7.cloned.1.call-start = ((), (), s32[]{:S(2)}) async-start(), calls=%async_computation.3 | async-start | bytes 7864320 | tf_op jit(solution)/shard_map/all_gather | solution.py:28
  7.3 158.4 %all-gather.5.cloned.1.call-start = ((), (), s32[]{:S(2)}) async-start(), calls=%async_computation.2 | async-start | bytes 9437184 | tf_op jit(solution)/shard_map/all_gather | solution.py:19
  11.4 224.7 %all-gather.9.cloned.1.call-start = ((), (), s32[]{:S(2)}) async-start(), calls=%async_computation.4 | async-start | bytes 7864320 | tf_op jit(solution)/shard_map/all_gather | solution.py:29
  12.1 295.5 %all-gather.11.cloned.1.call-start = ((), (), s32[]{:S(2)}) async-start(), calls=%async_computation.5 | async-start | bytes 7864320 | tf_op jit(solution)/shard_map/all_gather | solution.py:30
  12.7 511.2 %reduce-scatter.2.cloned.1.call-start = ((), (), s32[]{:S(2)}) async-start(), calls=%async_computation.6 | async-start | bytes 18874368 | tf_op jit(solution)/shard_map/reduce_scatter | solution.py:37
  165.6 11.8 %copy-start.2 = (bf16[2048,2048]{1,0:T(8,128)(2,1)S(1)}, bf16[2048,2048]{1,0:T(8,128)(2,1)}, u32[]{:S(2)}) copy-start(bf16[2048,2048]{1,0:T(8,128)(2,1)} %all-gather.5.cloned.1.call-done) | copy-start | bytes 25165828
  165.6 11.8 %copy-start.3 = (bf16[2,2048,768]{2,1,0:T(8,128)(2,1)S(1)}, bf16[2,2048,768]{2,1,0:T(8,128)(2,1)}, u32[]{:S(2)}) copy-start(bf16[2,2048,768]{2,1,0:T(8,128)(2,1)} %all-gather.7.cloned.1.call-done) | copy-start | bytes 18874372
Sparse Core Ops, SparseCore 0:
  9.2 72.7 all-gather.6
  83.6 82.0 all-gather.4
  167.5 68.5 all-gather.8
  237.7 69.8 all-gather.10
  355.6 168.1 reduce-scatter.1
where the time goes:
time: 533 us
  waiting for transfers between devices  433 us (81%)
  matrix products  68.2 us (13%)
  between operations  13.2 us (2%)
  blocking collectives  11.8 us (2%)
  other arithmetic  6.76 us (1%)
    reduce_scatter x1, waiting for transfers between devices, per_device(): combined = lax.psum_scatter(total, 'ep', scatter_dimension=0, tiled=True)  168 us
    all_gather x1, waiting for transfers between devices, per_device(): tokens = lax.all_gather(normed, 'ep', axis=0, tiled=True)  83.7 us
    all_gather x1, waiting for transfers between devices, per_device(): down_all = lax.all_gather(down_proj, 'fsdp', axis=2, tiled=True)  71.6 us
    all_gather x1, waiting for transfers between devices, per_device(): gate_all = lax.all_gather(gate_proj, 'fsdp', axis=1, tiled=True)  57.4 us
    all_gather x1, waiting for transfers between devices, per_device(): up_all = lax.all_gather(up_proj, 'fsdp', axis=1, tiled=True)  50.1 us
    dot_general x2, matrix products, per_device(): jnp.dot(act, down_all[e], preferred_element_type=jnp.float32)  47.9 us
    dot_general x2, matrix products, per_device(): gate = jnp.dot(tokens, gate_all[e], preferred_element_type=jnp.float32)  20.3 us
    all_to_all x1, blocking collectives, per_device(): lax.all_to_all(weights.reshape(weights.shape[0], lax.axis_size('ep'), loc...  11.8 us
  transfers between devices with their start and end apart: 5, of which 5 were waited for; matrix products, arithmetic and copies ran while one was open for 5% of the time, Pallas kernels for 0%

commit v1 on v0

--- a/solution.py
+++ b/solution.py
@@ -26,7 +26,7 @@
     ).reshape(tokens.shape[0], local_experts)
     total = 0.0
     gate_all = lax.all_gather(gate_proj, "fsdp", axis=1, tiled=True)
-    up_all = lax.all_gather(up_proj, "fsdp", axis=1, tiled=True)
+    up_all = jnp.concatenate(lax.all_gather(up_proj, "fsdp"), axis=1)
     down_all = lax.all_gather(down_proj, "fsdp", axis=2, tiled=True)
     for e in range(local_experts):
         gate = jnp.dot(tokens, gate_all[e], preferred_element_type=jnp.float32)

time: 533 us -> 532 us (level)
    all_gather x1, waiting for transfers between devices: 71.6 us -> 49.8 us  [per_device(): down_all = lax.all_gather(down_proj, 'fsdp', axis=2, tiled=True)]
    all_gather x1, waiting for transfers between devices: 57.4 us -> 66.9 us  [per_device(): gate_all = lax.all_gather(gate_proj, 'fsdp', axis=1, tiled=True)]
    all_gather x1, waiting for transfers between devices: 50.1 us -> 57.3 us  [per_device(): up_all = jnp.concatenate(lax.all_gather(up_proj, 'fsdp'), axis=1)]
  transfers between devices with their start and end apart: 5 -> 5, of which waited for: 5 -> 5; matrix products, arithmetic and copies ran while one was open for 5% -> 6% of each run, Pallas kernels for 0% -> 0%
where the time goes in v1:
time: 532 us
  waiting for transfers between devices  428 us (80%)
  matrix products  67.1 us (13%)
  between operations  13.2 us (2%)
  blocking collectives  11.8 us (2%)
  other arithmetic  6.76 us (1%)
    reduce_scatter x1, waiting for transfers between devices, per_device(): combined = lax.psum_scatter(total, 'ep', scatter_dimension=0, tiled=True)  168 us
    all_gather x1, waiting for transfers between devices, per_device(): tokens = lax.all_gather(normed, 'ep', axis=0, tiled=True)  83.7 us
    all_gather x1, waiting for transfers between devices, per_device(): gate_all = lax.all_gather(gate_proj, 'fsdp', axis=1, tiled=True)  66.9 us
    all_gather x1, waiting for transfers between devices, per_device(): up_all = jnp.concatenate(lax.all_gather(up_proj, 'fsdp'), axis=1)  57.3 us
    all_gather x1, waiting for transfers between devices, per_device(): down_all = lax.all_gather(down_proj, 'fsdp', axis=2, tiled=True)  49.8 us
    dot_general x2, matrix products, per_device(): jnp.dot(act, down_all[e], preferred_element_type=jnp.float32)  46.8 us
    dot_general x2, matrix products, per_device(): gate = jnp.dot(tokens, gate_all[e], preferred_element_type=jnp.float32)  20.3 us
    all_to_all x1, blocking collectives, per_device(): lax.all_to_all(weights.reshape(weights.shape[0], lax.axis_size('ep'), loc...  11.8 us
  transfers between devices with their start and end apart: 5, of which 5 were waited for; matrix products, arithmetic and copies ran while one was open for 6% of the time, Pallas kernels for 0%

profile of v1, /device:TPU:0, one launch (start us, length us, event | category | flops | bytes accessed | tf_op | source)
XLA Modules:
  0.0 532.0 jit_solution(10498136149874995461)
XLA Ops:
  6.5 0.0 copy-start
  6.5 0.0 copy-start.1
  6.5 0.0 all-gather.12.cloned.1.call-start
  6.5 0.7 all-gather.12.cloned.1.call-update
  7.3 0.0 all-gather.8.cloned.1.call-start
  7.3 0.7 all-gather.8.cloned.1.call-update
  8.0 0.0 all-gather.6.cloned.1.call-start
  8.1 1.5 fusion.5
  9.6 2.5 fusion.7
  12.1 0.0 all-gather.6.cloned.1.call-update
  12.1 0.0 all-gather.10.cloned.1.call-start
  12.2 0.5 all-gather.10.cloned.1.call-update
  12.7 0.0 reduce-scatter.2.cloned.1.call-start
  12.7 0.0 copy-done
  12.7 0.0 copy-done.1
  12.8 11.8 %all_to_all.15 = f32[256,8,2]{0,2,1:T(2,128)S(1)} all-to-all(f32[256,8,2]{0,2,1:T(2,128)S(1)} %reshape.27), channel_id=1, replica_groups=mesh['fsdp'=4,'ep'=8] {'ep'}, dimensions={1} | all-to-all | bytes 32768 | tf_op jit(solution)/shard_map/all_to_all | solution.py:20
  24.6 57.3 %all-gather.12.cloned.1.call-done = bf16[8,512,768]{2,1,0:T(8,128)(2,1)} async-done(((bf16[2,512,768]{2,1,0:T(8,128)(2,1)}), bf16[8,512,768]{2,1,0:T(8,128)(2,1)}) %all-gather.12.cloned.1.call-update) | async-done | bytes 6291472 | tf_op jit(solution)/shard_map/all_gather | solution.py:29
  82.0 5.0 fusion.10
  86.9 66.9 %all-gather.8.cloned.1.call-done = bf16[2,2048,768]{2,1,0:T(8,128)(2,1)} async-done(((bf16[2,512,768]{2,1,0:T(8,128)(2,1)}), bf16[2,2048,768]{2,1,0:T(8,128)(2,1)}) %all-gather.8.cloned.1.call-update) | async-done | bytes 6291472 | tf_op jit(solution)/shard_map/all_gather | solution.py:28
  153.9 83.7 %all-gather.6.cloned.1.call-done = bf16[2048,2048]{1,0:T(8,128)(2,1)} async-done(((bf16[256,2048]{1,0:T(8,128)(2,1)}), bf16[2048,2048]{1,0:T(8,128)(2,1)}) %all-gather.6.cloned.1.call-update) | async-done | bytes 8388624 | tf_op jit(solution)/shard_map/all_gather | solution.py:19
  237.5 0.0 copy-start.2
  237.5 0.0 copy-start.3
  237.5 11.8 %fusion.1 = f32[2048,768]{1,0:T(8,128)} fusion(bf16[2048,2048]{1,0:T(8,128)(2,1)} %all-gather.6.cloned.1.call-done, bf16[2,2048,768]{2,1,0:T(8,128)(2,1)} %all-gather.8.cloned.1.call-done), kind=kOutput, calls=%fused_computation.6 | convolution fusion | flops 6442450944 | bytes 17825792 | tf_op jit(solution)/shard_map/dot_general | solution.py:32
  249.3 0.0 copy-done.2
  249.3 0.0 copy-done.3
  249.3 8.5 %fusion.2 = f32[2048,768]{1,0:T(8,128)} fusion(bf16[2048,2048]{1,0:T(8,128)(2,1)S(1)} %copy-done.2, bf16[2,2048,768]{2,1,0:T(8,128)(2,1)S(1)} %copy-done.3), kind=kOutput, calls=%fused_computation.9 | convolution fusion | flops 6442450944 | bytes 17825792 | tf_op jit(solution)/shard_map/dot_general | solution.py:32
  257.8 49.8 %all-gather.10.cloned.1.call-done = bf16[2,768,2048]{2,1,0:T(8,128)(2,1)} async-done(((bf16[2,768,512]{2,1,0:T(8,128)(2,1)}), bf16[2,768,2048]{2,1,0:T(8,128)(2,1)}) %all-gather.10.cloned.1.call-update) | async-done | bytes 6291472 | tf_op jit(solution)/shard_map/all_gather | solution.py:30
  307.6 22.1 %fusion = bf16[2048,2048]{1,0:T(8,128)(2,1)} fusion(f32[2048,768]{1,0:T(8,128)} %fusion.2, bf16[2048,2048]{1,0:T(8,128)(2,1)} %all-gather.6.cloned.1.call-done, bf16[2048,768]{1,0:T(8,128)(2,1)} %bitcast.34, bf16[2,768,2048]{2,1,0:T(8,128)(2,1)} %all-gather.10.cloned.1.call-done), kind=kOutput, calls=%fused_computation.3 | convolution fusion | flops 12894339072 | bytes 29360128 | tf_op jit(solution)/shard_map/dot_general | solution.py:35
  329.7 24.7 %multiply_add_fusion = f32[2048,2048]{1,0:T(8,128)} fusion(f32[2048]{0:T(1024)S(1)} %bitcast.37, f32[2048]{0:T(1024)S(1)} %bitcast.36, bf16[2048,2048]{1,0:T(8,128)(2,1)} %fusion, f32[2048,768]{1,0:T(8,128)} %fusion.1, bf16[2048,2048]{1,0:T(8,128)(2,1)} %all-gather.6.cloned.1.call-done, bf16[2048,768]{1,0:T(8,128)(2,1)S(1)} %bitcast.33, ...), kind=kOutput, calls=%fused_computation | convolution fusion | flops 12919504896 | bytes 46153728 | tf_op jit(solution)/shard_map/dot_general | solution.py:35
  354.4 0.0 reduce-scatter.2.cloned.1.call-update
  354.5 168.3 %reduce-scatter.2.cloned.1.call-done = f32[256,2048]{1,0:T(8,128)} async-done(((f32[2048,2048]{1,0:T(8,128)}), f32[256,2048]{1,0:T(8,128)}) %reduce-scatter.2.cloned.1.call-update) | async-done | bytes 2097168 | tf_op jit(solution)/shard_map/reduce_scatter | solution.py:37
  522.8 2.7 convert_element_type.35
  (4 shorter events, 0.1 us)
Async XLA Ops:
  6.5 6.2 %copy-start = (f32[256,8]{0,1:T(8,128)S(1)}, f32[256,8]{0,1:T(8,128)}, u32[]{:S(2)}) copy-start(f32[256,8]{0,1:T(8,128)} %param.10) | copy-start | bytes 24580
  6.5 6.2 %copy-start.1 = (s32[256,8]{0,1:T(8,128)S(1)}, s32[256,8]{0,1:T(8,128)}, u32[]{:S(2)}) copy-start(s32[256,8]{0,1:T(8,128)} %param.9) | copy-start | bytes 24580
  6.5 75.4 %all-gather.12.cloned.1.call-start = ((), (), s32[]{:S(2)}) async-start(), calls=%async_computation.6 | async-start | bytes 7864320 | tf_op jit(solution)/shard_map/all_gather | solution.py:29
  7.3 146.6 %all-gather.8.cloned.1.call-start = ((), (), s32[]{:S(2)}) async-start(), calls=%async_computation.3 | async-start | bytes 7864320 | tf_op jit(solution)/shard_map/all_gather | solution.py:28
  8.0 229.5 %all-gather.6.cloned.1.call-start = ((), (), s32[]{:S(2)}) async-start(), calls=%async_computation.2 | async-start | bytes 9437184 | tf_op jit(solution)/shard_map/all_gather | solution.py:19
  12.1 295.5 %all-gather.10.cloned.1.call-start = ((), (), s32[]{:S(2)}) async-start(), calls=%async_computation.4 | async-start | bytes 7864320 | tf_op jit(solution)/shard_map/all_gather | solution.py:30
  12.7 510.1 %reduce-scatter.2.cloned.1.call-start = ((), (), s32[]{:S(2)}) async-start(), calls=%async_computation.5 | async-start | bytes 18874368 | tf_op jit(solution)/shard_map/reduce_scatter | solution.py:37
  237.5 11.8 %copy-start.2 = (bf16[2048,2048]{1,0:T(8,128)(2,1)S(1)}, bf16[2048,2048]{1,0:T(8,128)(2,1)}, u32[]{:S(2)}) copy-start(bf16[2048,2048]{1,0:T(8,128)(2,1)} %all-gather.6.cloned.1.call-done) | copy-start | bytes 25165828
  237.5 11.8 %copy-start.3 = (bf16[2,2048,768]{2,1,0:T(8,128)(2,1)S(1)}, bf16[2,2048,768]{2,1,0:T(8,128)(2,1)}, u32[]{:S(2)}) copy-start(bf16[2,2048,768]{2,1,0:T(8,128)(2,1)} %all-gather.8.cloned.1.call-done) | copy-start | bytes 18874372
Sparse Core Ops, SparseCore 0:
  9.2 72.7 all-gather.11
  83.8 70.0 all-gather.7
  155.5 82.0 all-gather.5
  239.2 68.3 all-gather.9
  354.6 168.1 reduce-scatter.1
